TPU v7x, 256 devices: a whole 4x4x8 slice. The times are simulated.
256 devices in a mesh: row: 16 (over z_lo, y), col: 16 (over z_hi, x, core).
Axes of the slice: x: 4, y: 4, z: 8 (z_hi: 2, z_lo: 4; z = z_hi * 4 + z_lo), core: 2. Of those that a mesh axis runs over, the one named last changes fastest.
Arguments:
- orbitals: float32 [2048, 28672], P(('row', 'col')), may hold values from -0.03125 to 0.03125
- applied: float32 [2048, 28672], P(('row', 'col')), may hold values from -24 to 24
Outputs:
- hamiltonian: float32 [2048, 2048], P('col', 'row')
- intersection: float32 [2048, 2048], P('col', 'row')
All inputs are finite; a program needn't handle non-finite values.
Results may differ from a plain program's by a relative error of at most 0.000098.
Values sent between devices are 32-bit elements; how exact they have to be, the bound alone decides.
A program may use at most 64 MiB of HBM per device.

v0:
```python
import jax
import jax.numpy as jnp
from jax import lax
from jax.sharding import PartitionSpec as P


def sent_together(arrays, axis, dim, along):
    both = jnp.concatenate(arrays, axis=along)
    result, at, done = (lax.psum_scatter(both, axis, scatter_dimension=dim, tiled=True), 0, [])
    for a in arrays:
        done.append(lax.slice_in_dim(result, at, at + a.shape[along], axis=along))
        at += a.shape[along]
    return tuple(done)


def product(left, right):
    return lax.dot_general(
        left,
        right,
        (((1,), (1,)), ((), ())),
        precision=lax.Precision.HIGHEST,
        preferred_element_type=jnp.float32,
    )


def shards(orbitals, applied):
    mine_orb, mine_app = (
        lax.all_to_all(orbitals, "col", split_axis=1, concat_axis=0, tiled=True),
        lax.all_to_all(applied, "col", split_axis=1, concat_axis=0, tiled=True),
    )
    every_orb = lax.all_gather(mine_orb, "row", axis=0, tiled=True)
    ham_part = product(every_orb, mine_app)
    ovl_part = product(every_orb, mine_orb)
    hamiltonian, intersection = sent_together((ham_part, ovl_part), "col", 0, 1)
    return (hamiltonian, intersection)


def solution(mesh):
    placed = (P(("row", "col"), None), P(("row", "col"), None))
    return jax.shard_map(
        shards,
        mesh=mesh,
        in_specs=placed,
        out_specs=(P("col", "row"), P("col", "row")),
        check_vma=False,
    )
```

profile of v0, /device:TPU:8, one launch (start us, length us, event | category | flops | bytes accessed | tf_op | source)
XLA Modules:
  0.0 355.5 jit_solution(10867969578513426620)
XLA Ops:
  7.2 0.0 all-gather.2.cloned.1.call-start
  7.2 32.4 %all_to_all.38 = f32[8,16,1792]{2,0,1:T(8,128)} all-to-all(f32[8,16,1792]{2,0,1:T(8,128)} %bitcast.15), channel_id=1, replica_groups=mesh['row'=16,'col'=16] {'col'}, dimensions={1} | all-to-all | bytes 1835008 | tf_op jit(solution)/shard_map/all_to_all | solution.py:28
  39.6 0.0 all-gather.2.cloned.1.call-update
  39.7 3.6 %all-to-all-start.1 = ((f32[8,16,1792]{2,0,1:T(8,128)}), f32[8,16,1792]{2,0,1:T(8,128)S(1)}, u32[]{:S(2)}, u32[]{:S(2)}) async-start(f32[8,16,1792]{2,0,1:T(8,128)} %bitcast.16), calls=%async_computation.1 | async-start | bytes 1835008 | tf_op jit(solution)/shard_map/all_to_all | solution.py:29
  43.3 0.0 reduce-scatter.2.cloned.1.call-start
  43.4 173.2 %all-gather.2.cloned.1.call-done = f32[2048,1792]{1,0:T(8,128)} async-done(((f32[128,1792]{1,0:T(8,128)}), f32[2048,1792]{1,0:T(8,128)}) %all-gather.2.cloned.1.call-update) | async-done | bytes 14680080 | tf_op jit(solution)/shard_map/all_gather | solution.py:31
  216.6 18.5 %fusion.2 = f32[2048,128]{0,1:T(8,128)S(1)} fusion(f32[2048,1792]{1,0:T(8,128)} %all-gather.2.cloned.1.call-done, f32[8,16,1792]{2,0,1:T(8,128)} %all_to_all.38), kind=kOutput, calls=%fused_computation.3 | convolution fusion | flops 5637144576 | bytes 16646144 | tf_op jit(solution)/shard_map/dot_general | solution.py:17
  235.1 0.0 all-to-all-done.1
  235.2 18.3 %fusion = f32[2048,128]{0,1:T(8,128)S(1)} fusion(f32[2048,1792]{1,0:T(8,128)} %all-gather.2.cloned.1.call-done, f32[8,16,1792]{2,0,1:T(8,128)S(1)} %all-to-all-done.1), kind=kOutput, calls=%fused_computation.1 | convolution fusion | flops 5637144576 | bytes 16646144 | tf_op jit(solution)/shard_map/dot_general | solution.py:17
  253.5 1.5 pad_maximum_fusion
  255.0 0.0 reduce-scatter.2.cloned.1.call-update
  255.0 91.3 %reduce-scatter.2.cloned.1.call-done = f32[128,256]{0,1:T(8,128)} async-done(((f32[2048,256]{0,1:T(8,128)}), f32[128,256]{0,1:T(8,128)}) %reduce-scatter.2.cloned.1.call-update) | async-done | bytes 131088 | tf_op jit(solution)/shard_map/reduce_scatter | solution.py:9
  346.4 0.9 fusion.4
  347.2 0.7 copy.5
  348.0 0.7 copy.4
Async XLA Ops:
  7.2 209.5 %all-gather.2.cloned.1.call-start = ((), (), s32[]{:S(2)}) async-start(), calls=%async_computation.3 | async-start | bytes 15597568 | tf_op jit(solution)/shard_map/all_gather | solution.py:31
  39.7 195.5 %all-to-all-start.1 = ((f32[8,16,1792]{2,0,1:T(8,128)}), f32[8,16,1792]{2,0,1:T(8,128)S(1)}, u32[]{:S(2)}, u32[]{:S(2)}) async-start(f32[8,16,1792]{2,0,1:T(8,128)} %bitcast.16), calls=%async_computation.1 | async-start | bytes 1835008 | tf_op jit(solution)/shard_map/all_to_all | solution.py:29
  43.3 303.0 %reduce-scatter.2.cloned.1.call-start = ((), (), s32[]{:S(2)}) async-start(), calls=%async_computation.4 | async-start | bytes 2228224 | tf_op jit(solution)/shard_map/reduce_scatter | solution.py:9
Sparse Core Ops, SparseCore 0:
  39.8 176.7 all-gather.1
  255.1 91.1 reduce-scatter.1
where the time goes:
time: 356 us
  waiting for transfers between devices  265 us (74%)
  matrix products  36.8 us (10%)
  blocking collectives  32.4 us (9%)
  between operations  14.1 us (4%)
  starting transfers between devices  3.73 us (1%)
    all_gather x1, waiting for transfers between devices, shards(): every_orb = lax.all_gather(mine_orb, 'row', axis=0, tiled=True)  173 us
    reduce_scatter x1, waiting for transfers between devices, sent_together(): lax.psum_scatter(both, axis, scatter_dimension=dim, tiled=True)  91.3 us
    dot_general x2, matrix products, product(): lax.dot_general(left, right, (((1,), (1,)), ((), ())), precision=lax.Prec...  36.8 us
    all_to_all x1, blocking collectives, shards(): lax.all_to_all(orbitals, 'col', split_axis=1, concat_axis=0, tiled=True)  32.4 us
  transfers between devices with their start and end apart: 3, of which 2 were waited for; matrix products, arithmetic and copies ran while one was open for 5% of the time, Pallas kernels for 0%

commit v1 on v0

--- a/solution.py
+++ b/solution.py
@@ -28,7 +28,10 @@
         lax.all_to_all(orbitals, "col", split_axis=1, concat_axis=0, tiled=True),
         lax.all_to_all(applied, "col", split_axis=1, concat_axis=0, tiled=True),
     )
-    every_orb = lax.all_gather(mine_orb, "row", axis=0, tiled=True)
+    count = lax.axis_size("row")
+    parts = jnp.stack([mine_orb for _ in range(count)])
+    parts = lax.all_to_all(parts, "row", split_axis=0, concat_axis=0)
+    every_orb = jnp.concatenate(parts, axis=0)
     ham_part = product(every_orb, mine_app)
     ovl_part = product(every_orb, mine_orb)
     hamiltonian, intersection = sent_together((ham_part, ovl_part), "col", 0, 1)

time: 356 us -> 516 us (1.45)
  blocking collectives: 32.4 us -> 362 us
  waiting for transfers between devices: 265 us -> 93.5 us
    all_to_all x0 -> x1, blocking collectives: none -> 330 us  [shards(): parts = lax.all_to_all(parts, 'row', split_axis=0, concat_axis=0)]
    all_gather x1 -> x0, waiting for transfers between devices: 173 us -> none  [shards(): every_orb = lax.all_gather(mine_orb, 'row', axis=0, tiled=True)]
  transfers between devices with their start and end apart: 3 -> 2, of which waited for: 2 -> 2; matrix products, arithmetic and copies ran while one was open for 5% -> 4% of each run, Pallas kernels for 0% -> 0%
where the time goes in v1:
time: 516 us; the launch traced here: 515 us
  blocking collectives  362 us (70%)
  waiting for transfers between devices  93.5 us (18%)
  matrix products  36.7 us (7%)
  between operations  14.1 us (3%)
    all_to_all x1, blocking collectives, shards(): parts = lax.all_to_all(parts, 'row', split_axis=0, concat_axis=0)  330 us
    reduce_scatter x1, waiting for transfers between devices, sent_together(): lax.psum_scatter(both, axis, scatter_dimension=dim, tiled=True)  92.8 us
    dot_general x2, matrix products, product(): lax.dot_general(left, right, (((1,), (1,)), ((), ())), precision=lax.Prec...  36.7 us
    all_to_all x1, blocking collectives, shards(): lax.all_to_all(orbitals, 'col', split_axis=1, concat_axis=0, tiled=True)  32.3 us
  transfers between devices with their start and end apart: 2, of which 2 were waited for; matrix products, arithmetic and copies ran while one was open for 4% of the time, Pallas kernels for 0%

profile of v1, /device:TPU:8, one launch (start us, length us, event | category | flops | bytes accessed | tf_op | source)
XLA Modules:
  0.0 515.3 jit_solution(2663192728453900688)
XLA Ops:
  7.2 32.3 %all_to_all.40 = f32[8,16,1792]{2,0,1:T(8,128)S(1)} all-to-all(f32[8,16,1792]{2,0,1:T(8,128)} %bitcast.18), channel_id=1, replica_groups=mesh['row'=16,'col'=16] {'col'}, dimensions={1} | all-to-all | bytes 1835008 | tf_op jit(solution)/shard_map/all_to_all | solution.py:28
  39.5 1.4 stack.5
  40.9 329.9 %all_to_all.41 = f32[16,128,1792]{2,1,0:T(8,128)} all-to-all(f32[16,128,1792]{2,1,0:T(8,128)S(1)} %stack.5), channel_id=1, replica_groups=mesh['row'=16,'col'=16] {'row'}, dimensions={0} | all-to-all | bytes 29360128 | tf_op jit(solution)/shard_map/all_to_all | solution.py:33
  370.8 3.6 all-to-all-start.2
  374.4 0.0 reduce-scatter.2.cloned.1.call-start
  374.5 18.3 %fusion.2 = f32[2048,128]{0,1:T(8,128)S(1)} fusion(f32[2048,1792]{1,0:T(8,128)} %bitcast.15, f32[8,16,1792]{2,0,1:T(8,128)S(1)} %all_to_all.40), kind=kOutput, calls=%fused_computation.3 | convolution fusion | flops 5637144576 | bytes 16646144 | tf_op jit(solution)/shard_map/dot_general | solution.py:17
  392.8 0.7 all-to-all-done.2
  393.5 18.3 %fusion = f32[2048,128]{0,1:T(8,128)S(1)} fusion(f32[2048,1792]{1,0:T(8,128)} %bitcast.16, f32[8,16,1792]{2,0,1:T(8,128)S(1)} %all-to-all-done.2), kind=kOutput, calls=%fused_computation.1 | convolution fusion | flops 5637144576 | bytes 16646144 | tf_op jit(solution)/shard_map/dot_general | solution.py:17
  411.9 1.5 pad_maximum_fusion
  413.3 0.0 reduce-scatter.2.cloned.1.call-update
  413.4 92.8 %reduce-scatter.2.cloned.1.call-done = f32[128,256]{0,1:T(8,128)} async-done(((f32[2048,256]{0,1:T(8,128)}), f32[128,256]{0,1:T(8,128)}) %reduce-scatter.2.cloned.1.call-update) | async-done | bytes 131088 | tf_op jit(solution)/shard_map/reduce_scatter | solution.py:9
  506.1 0.9 fusion.4
  507.0 0.7 copy.4
  507.8 0.7 copy.5
Async XLA Ops:
  370.8 22.7 %all-to-all-start.2 = ((f32[8,16,1792]{2,0,1:T(8,128)}), f32[8,16,1792]{2,0,1:T(8,128)S(1)}, u32[]{:S(2)}, u32[]{:S(2)}) async-start(f32[8,16,1792]{2,0,1:T(8,128)} %bitcast.4), calls=%async_computation.2 | async-start | bytes 1835008 | tf_op jit(solution)/shard_map/all_to_all | solution.py:29
  374.4 131.7 %reduce-scatter.2.cloned.1.call-start = ((), (), s32[]{:S(2)}) async-start(), calls=%async_computation.4 | async-start | bytes 2228224 | tf_op jit(solution)/shard_map/reduce_scatter | solution.py:9
Sparse Core Ops, SparseCore 0:
  413.5 92.6 reduce-scatter.1
